TPU v7x, 256 devices: a whole 4x4x8 slice. The times are simulated.
256 devices in a mesh: level: 2 (over x_hi), gx: 16 (over x_lo, z), gy: 8 (over y, core).
Axes of the slice: x: 4 (x_hi: 2, x_lo: 2; x = x_hi * 2 + x_lo), y: 4, z: 8, core: 2. Of those that a mesh axis runs over, the one named last changes fastest.
Arguments:
- u_init: float32 [128, 256, 256], P('gx', 'gy'), may hold values from -6 to 6
- v_init: float32 [128, 256, 256], P('gx', 'gy'), may hold values from -6 to 6
- speed_sq: float32 [128, 256, 256], P('gx', 'gy'), may hold values from 0.25 to 1
Outputs:
- final_u: float32 [2, 128, 256, 256], P('level', 'gx', 'gy')
- final_v: float32 [2, 128, 256, 256], P('level', 'gx', 'gy')
All inputs are finite; a program needn't handle non-finite values.
Results may differ from a plain program's by a relative error of at most 0.00002.
Values sent between devices are 32-bit elements; how exact they have to be, the bound alone decides.
A program may use at most 64 MiB of HBM per device.

v0:
```python
import functools

import jax
import jax.numpy as jnp
from jax import lax
from jax.experimental import pallas as pl
from jax.experimental.pallas import tpu as pltpu
from jax.sharding import PartitionSpec as P


H = 0.12
D = 0.05
W1 = 4.0 / 3.0
W2 = -1.0 / 12.0
ROUNDS = 3
MESH = pl.DeviceIdType.MESH
F32 = jnp.float32
XO, YO = 4, 8
OWN = slice(YO, YO + 32)
LO, HI = slice(0, 8), slice(40, 48)
DIAG = ((1, 1), (1, -1), (-1, 1), (-1, -1))


def rows(shape):
    return lax.broadcasted_iota(jnp.int32, shape, len(shape) - 2)


def turn(x, n):
    return pltpu.roll(x, n % 8, x.ndim - 2)


def from_below(c):
    r = rows(c.shape)
    return jnp.where(r == 0, W1 * turn(c, 1), 0.0) + jnp.where(r < 2, W2 * turn(c, 2), 0.0)


def from_above(c):
    r = rows(c.shape)
    return jnp.where(r == 7, W1 * turn(c, 7), 0.0) + jnp.where(r >= 6, W2 * turn(c, 6), 0.0)


def z_sums(a, b):
    lane = lax.broadcasted_iota(jnp.int32, a.shape, a.ndim - 1)
    ax = a.ndim - 1

    def shifted(n, mask):
        ra, rb = pltpu.roll(a, n % 128, ax), pltpu.roll(b, n % 128, ax)
        return jnp.where(mask, rb, ra), jnp.where(mask, ra, rb)

    l1, l2 = shifted(1, lane < 1), shifted(2, lane < 2)
    r1, r2 = shifted(127, lane >= 127), shifted(126, lane >= 126)
    return [(l1[i] + r1[i], l2[i] + r2[i]) for i in range(2)]


def lap(ref, p, lo, n, planes=None):
    at = (lambda q: q) if planes is None else (lambda q: pl.ds(q, planes))
    mid = [ref[at(p), f, lo : lo + n, :] for f in range(2)]
    zs = z_sums(*mid)
    out = []
    for f in range(2):
        near = zs[f][0] + ref[at(p - 1), f, lo : lo + n, :] + ref[at(p + 1), f, lo : lo + n, :]
        near = near + ref[at(p), f, lo - 1 : lo - 1 + n, :] + ref[at(p), f, lo + 1 : lo + 1 + n, :]
        far = zs[f][1] + ref[at(p - 2), f, lo : lo + n, :] + ref[at(p + 2), f, lo : lo + n, :]
        far = far + ref[at(p), f, lo - 2 : lo - 2 + n, :] + ref[at(p), f, lo + 2 : lo + 2 + n, :]
        out.append(W1 * near + (W2 * far - 7.5 * mid[f]))
    return out


def kernel(u_hbm, v_hbm, s_hbm, ou_hbm, ov_hbm, IU, I0, I1, I2, T0, T1, T2, TU, S, U, acc, A7, eW, eE, eS, eN, gW, gE, gS, gN,
           cs, cr, ob, lsem, ssem, rsem):
    level = lax.axis_index("level")
    gx, gy = lax.axis_index("gx"), lax.axis_index("gy")
    nx, ny = lax.axis_size("gx"), lax.axis_size("gy")

    def peer(dx, dy):
        return (level, lax.rem(gx + dx + nx, nx), lax.rem(gy + dy + ny, ny))

    around = ((1, 0), (-1, 0), (0, 1), (0, -1)) + DIAG
    barrier = pltpu.get_barrier_semaphore()
    for d in around:
        pl.semaphore_signal(barrier, 1, device_id=peer(*d), device_id_type=MESH)

    loads = []
    for src, dsts in ((v_hbm, ((I0, 2), (T0.at[0], XO))), (u_hbm, ((IU, 2), (TU, XO))), (s_hbm, ((S, XO),))):
        for dst, off in dsts:
            for f in range(2):
                copy = pltpu.make_async_copy(
                    src.at[:, :, 128 * f : 128 * f + 128], dst.at[off : off + 8, f, OWN, :], lsem.at[len(loads)]
                )
                copy.start()
                loads.append(copy)

    zero = jnp.zeros((2, 2, 48, 128), F32)
    for ref in (IU, I0, I1, I2):
        ref[0:2] = zero
        ref[10:12] = zero
        for sl in (LO, HI):
            ref[2:10, :, sl, :] = jnp.zeros((8, 2, 8, 128), F32)
    for ref in (eW, eE):
        ref[...] = jnp.zeros((6, 2, 48, 128), F32)
    for ref in (eS, eN):
        ref[...] = jnp.zeros((12, 2, 24, 128), F32)

    for copy in loads:
        copy.wait()
    pl.semaphore_wait(barrier, len(around))

    def send(r, slot, src, dst, dx, dy):
        copy = pltpu.make_async_remote_copy(
            src_ref=src, dst_ref=dst, send_sem=ssem.at[r, slot], recv_sem=rsem.at[r, slot],
            device_id=peer(dx, dy), device_id_type=MESH,
        )
        copy.start()
        return copy

    def send_x(r, slot, src, off, dst):
        return [
            send(r, slot, src.at[off + 6 : off + 8, :, OWN, :], dst.at[XO - 2 : XO, :, OWN, :], 1, 0),
            send(r, slot + 1, src.at[off : off + 2, :, OWN, :], dst.at[XO + 8 : XO + 10, :, OWN, :], -1, 0),
        ]

    def send_y(r, slot, src, off, dst):
        return [
            send(r, slot, src.at[off : off + 8, :, 32:40, :], dst.at[XO : XO + 8, :, LO, :], 0, 1),
            send(r, slot + 1, src.at[off : off + 8, :, 8:16, :], dst.at[XO : XO + 8, :, HI, :], 0, -1),
        ]

    def pack4(a, b, sy):
        r = rows(a.shape)
        return jnp.where(r >= 4 if sy > 0 else r < 4, b, turn(a, 4))

    def pack2(items, sy):
        r = rows(items[0].shape)
        out = items[0]
        for i in range(1, 4):
            first = ((6 if sy > 0 else 0) + 2 * i) % 8
            out = jnp.where((r == first) | (r == first + 1), turn(items[i], 2 * i), out)
        return out

    def corner(sx, sy):
        near = (6, 7) if sx > 0 else (0, 1)
        far = (4, 5) if sx > 0 else (2, 3)
        return near, far, (slice(32, 40) if sy > 0 else slice(8, 16))

    def corner_in(sx, sy):
        near = (XO - 2, XO - 1) if sx > 0 else (XO + 8, XO + 9)
        far = (XO - 4, XO - 3) if sx > 0 else (XO + 10, XO + 11)
        return near, far, (LO if sy > 0 else HI)

    waiting = []
    for r in range(ROUNDS):
        first, last = r == 0, r == ROUNDS - 1
        t0, t1, t2 = T0.at[r], T1.at[r], T2.at[r]
        sent = []
        x0 = send_x(r, 0, I0, 2, t0)
        y0 = send_y(r, 2, I0, 2, t0)
        extra = []
        if first:
            extra = send_x(r, 16, IU, 2, TU) + send_y(r, 18, IU, 2, TU)
            extra += send_x(r, 20, S, XO, S) + send_y(r, 22, S, XO, S)
            for i, sl in enumerate((slice(8, 16), slice(32, 40))):
                extra.append(send(r, 24 + 2 * i, S.at[XO + 4 : XO + 6, :, sl, :], S.at[XO - 4 : XO - 2, :, sl, :], 1, 0))
                extra.append(send(r, 25 + 2 * i, S.at[XO + 2 : XO + 4, :, sl, :], S.at[XO + 10 : XO + 12, :, sl, :], -1, 0))

            def start(p, c):
                for f, value in enumerate(lap(IU, p + 2, YO, 32)):
                    U[p, f] = value
                    acc[p, f] = IU[p + 2, f, OWN, :]
                return c

            lax.fori_loop(0, 8, start, 0)

        def alone1(p, c):
            for f, value in enumerate(lap(I0, p + 2, YO, 32)):
                I1[p + 2, f, OWN, :] = I0[p + 2, f, OWN, :] + H * (S[p + XO, f, OWN, :] * U[p, f] + D * value)
                U[p, f] = U[p, f] + H * value
            return c

        lax.fori_loop(0, 8, alone1, 0)
        x1 = send_x(r, 4, I1, 2, t1)
        y1 = send_y(r, 6, I1, 2, t1)
        diag = []
        for i, (sx, sy) in enumerate(DIAG):
            near, far, sl = corner(sx, sy)
            cs[i, 0] = pack4(*[I0[q + 2, :, sl, :] for q in near], sy)
            cs[i, 1] = pack2([I0[q + 2, :, sl, :] for q in far] + [I1[q + 2, :, sl, :] for q in near], sy)
            if first:
                cs[i, 2] = pack4(*[IU[q + 2, :, sl, :] for q in near], sy)
                cs[i, 3] = pack2([IU[q + 2, :, sl, :] for q in far] + [S[q + XO, :, sl, :] for q in near], sy)
            n = 4 if first else 2
            diag.append(send(r, 12 + i, cs.at[i, 0:n], cr.at[r, i, 0:n], sx, sy))

        def alone2(p, c):
            for f, value in enumerate(lap(I1, p + 2, YO, 32)):
                I2[p + 2, f, OWN, :] = I1[p + 2, f, OWN, :] + H * (S[p + XO, f, OWN, :] * U[p, f] + D * value)
            return c

        lax.fori_loop(0, 8, alone2, 0)
        x2 = send_x(r, 8, I2, 2, t2)
        y2 = send_y(r, 10, I2, 2, t2)

        for copy in y0 + x0 + extra:
            copy.wait()

        def own1(p, c):
            for f in range(2):
                for sl, cross, g in ((slice(8, 16), from_below, LO), (slice(32, 40), from_above, HI)):
                    k = slice(sl.start - YO, sl.stop - YO)
                    xv = cross(t0[p + XO, f, g, :])
                    add, grow = H * D * xv, H * xv
                    if first:
                        xu = cross(TU[p + XO, f, g, :])
                        add, grow = add + H * (S[p + XO, f, sl, :] * xu), grow + xu
                    t1[p + XO, f, sl, :] = I1[p + 2, f, sl, :] + add
                    U[p, f, k, :] = U[p, f, k, :] + grow
                t1[p + XO, f, 16:32, :] = I1[p + 2, f, 16:32, :]
            return c

        lax.fori_loop(0, 8, own1, 0)

        def cross_x(ref, x, sl):
            if x in (0, 8):
                a, b = (-1, -2) if x == 0 else (7, 6)
            elif x in (-1, 7):
                a, b = (0, 1) if x == -1 else (8, 9)
            else:
                return W2 * ref[{1: -1, -2: 0, 6: 8, 9: 7}[x] + XO, :, sl, :]
            return W1 * ref[a + XO, :, sl, :] + W2 * ref[b + XO, :, sl, :]

        for x in (0, 1, 6, 7):
            xv = cross_x(t0, x, OWN)
            add, grow = H * D * xv, H * xv
            if first:
                xu = cross_x(TU, x, OWN)
                add, grow = add + H * (S[x + XO, :, OWN, :] * xu), grow + xu
            t1[x + XO, :, OWN, :] = t1[x + XO, :, OWN, :] + add
            U[x] = U[x] + grow

        for copy in diag:
            copy.wait()
        for i, (sx, sy) in enumerate(DIAG):
            near, far, sl = corner_in(sx, sy)
            for k, ref in ((0, t0), (2, TU))[: 2 if first else 1]:
                ref[near[1], :, sl, :] = cr[r, i, k]
                ref[near[0], :, sl, :] = turn(cr[r, i, k], 4)
                ref[far[0], :, sl, :] = cr[r, i, k + 1]
                ref[far[1], :, sl, :] = turn(cr[r, i, k + 1], 6)
            for k, ref in ((1, t1), (3, S))[: 2 if first else 1]:
                ref[near[0], :, sl, :] = turn(cr[r, i, k], 4)
                ref[near[1], :, sl, :] = turn(cr[r, i, k], 2)

        def both(cross, *where):
            xv = cross(t0)
            e, g = H * D * xv, H * xv
            if first:
                xu = cross(TU)
                e, g = e + H * (S[where] * xu), g + xu
            return e, g

        every = slice(None)
        for side, (e_ref, g_ref, near, far) in enumerate(
            ((eW, gW, (-2, -1), (-4, -3)), (eE, gE, (8, 9), (10, 11)))
        ):
            base = -4 if side == 0 else 6
            for x in near:
                e, g = both(lambda ref: cross_x(ref, x, OWN), x + XO, every, OWN)
                e_ref[x - base, :, OWN, :] = e
                g_ref[x - near[0]] = g
            for x in near + far:
                for sl, cross, g_sl in ((slice(8, 16), from_below, LO), (slice(32, 40), from_above, HI)):
                    e, g = both(lambda ref: cross(ref[x + XO, :, g_sl, :]), x + XO, every, sl)
                    if x in near:
                        k = slice(sl.start - YO, sl.stop - YO)
                        e_ref[x - base, :, sl, :] = e_ref[x - base, :, sl, :] + e
                        g_ref[x - near[0], :, k, :] = g_ref[x - near[0], :, k, :] + g
                    else:
                        e_ref[x - base, :, sl, :] = e
        sides = ((eS, gS, LO, from_above, slice(8, 16)), (eN, gN, HI, from_below, slice(32, 40)))
        mid = slice(XO, XO + 8)
        for e_ref, g_ref, sl, cross, o_sl in sides:
            e, g = both(lambda ref: cross(ref[mid, :, o_sl, :]), mid, every, sl)
            e_ref[2:10, :, 8:16, :] = e
            g_ref[...] = g
            for x in (0, 1, 6, 7):
                e, g = both(lambda ref: cross_x(ref, x, sl), x + XO, every, sl)
                e_ref[x + 2, :, 8:16, :] = e_ref[x + 2, :, 8:16, :] + e
                g_ref[x] = g_ref[x] + g
            for x in (-2, -1, 8, 9):
                e, g = both(lambda ref: cross_x(ref, x, sl) + cross(ref[x + XO, :, o_sl, :]), x + XO, every, sl)
                t1[x + XO, :, sl, :] = t1[x + XO, :, sl, :] + e

        for copy in y1 + x1:
            copy.wait()
        for e_ref, x, k in ((eW, XO - 2, 2), (eE, XO + 8, 2)):
            t1[x : x + 2, :, OWN, :] = t1[x : x + 2, :, OWN, :] + e_ref[k : k + 2, :, OWN, :]
        for e_ref, g_ref, sl, cross, o_sl in sides:
            t1[mid, :, sl, :] = t1[mid, :, sl, :] + e_ref[2:10, :, 8:16, :]

        def own2(p, c):
            for f, value in enumerate(lap(t1, p + XO, YO, 32)):
                s, u = S[p + XO, f, OWN, :], U[p, f]
                a = s * u + D * value
                t2[p + XO, f, OWN, :] = t1[p + XO, f, OWN, :] + H * a
                if last:
                    A7[p, f] = a
                U[p, f] = u + H * value
            return c

        lax.fori_loop(0, 8, own2, 0)

        for e_ref, g_ref, near, base in ((eW, gW, (-2, -1), -4), (eE, gE, (8, 9), 6)):
            for x in near:
                value = lap(e_ref, x - base, YO, 32) if True else None
                cx = cross_x(t1, x, OWN)
                for f in range(2):
                    full = value[f] + cx[f]
                    low = full[0:8] + from_below(t1[x + XO, f, LO, :])
                    high = full[24:32] + from_above(t1[x + XO, f, HI, :])
                    full = jnp.concatenate([low, full[8:24], high], axis=0)
                    e = e_ref[x - base, f, OWN, :] + H * (S[x + XO, f, OWN, :] * g_ref[x - near[0], f] + D * full)
                    g_ref[x - near[0], f] = e
        for e_ref, g_ref, sl, cross, o_sl in sides:
            value = lap(e_ref, 2, 8, 8, planes=8)
            for f in range(2):
                full = value[f] + cross(t1[mid, f, o_sl, :])
                e = e_ref[2:10, f, 8:16, :] + H * (S[mid, f, sl, :] * g_ref[:, f] + D * full)
                g_ref[:, f] = e
            for x in (0, 1, 6, 7):
                g_ref[x] = g_ref[x] + H * D * cross_x(t1, x, sl)

        for copy in y2 + x2:
            copy.wait()
        for g_ref, x in ((gW, XO - 2), (gE, XO + 8)):
            t2[x : x + 2, :, OWN, :] = t2[x : x + 2, :, OWN, :] + g_ref[...]
        for e_ref, g_ref, sl, cross, o_sl in sides:
            t2[mid, :, sl, :] = t2[mid, :, sl, :] + g_ref[...]

        if not last:
            nxt = T0.at[r + 1]

            def own3(p, c):
                for f, value in enumerate(lap(t2, p + XO, YO, 32)):
                    u, mine = U[p, f], t2[p + XO, f, OWN, :]
                    new = mine + H * (S[p + XO, f, OWN, :] * u + D * value)
                    I0[p + 2, f, OWN, :] = new
                    nxt[p + XO, f, OWN, :] = new
                    U[p, f] = u + H * value
                    acc[p, f] = acc[p, f] + H * (t0[p + XO, f, OWN, :] + t1[p + XO, f, OWN, :] + mine)
                return c

            lax.fori_loop(0, 8, own3, 0)
        else:
            raised = level == 1

            def finish(p, c):
                for f, value in enumerate(lap(t2, p + XO, YO, 32)):
                    v7, v8 = t1[p + XO, f, OWN, :], t2[p + XO, f, OWN, :]
                    a8 = S[p + XO, f, OWN, :] * U[p, f] + D * value
                    u8 = acc[p, f] + H * (t0[p + XO, f, OWN, :] + v7)
                    ob[0, p, f] = jnp.where(raised, u8 + 4 * H * (v8 - v7), u8)
                    ob[1, p, f] = jnp.where(raised, v8 + 4 * H * (a8 - A7[p, f]), v8)
                return c

            lax.fori_loop(0, 8, finish, 0)
    stores = []
    for i, dst in enumerate((ou_hbm, ov_hbm)):
        for f in range(2):
            copy = pltpu.make_async_copy(ob.at[i, :, f], dst.at[0, :, :, 128 * f : 128 * f + 128], lsem.at[2 * i + f])
            copy.start()
            stores.append(copy)
    for copy in stores:
        copy.wait()


def body(u, v, s):
    ext, alone, block = (16, 2, 48, 128), (12, 2, 48, 128), (8, 2, 32, 128)
    vm = lambda *shape: pltpu.VMEM(shape, F32)
    scratch = [vm(*alone)] * 4 + [vm(ROUNDS, *ext)] * 3 + [vm(*ext)] * 2 + [vm(*block)] * 3
    scratch += [vm(6, 2, 48, 128)] * 2 + [vm(12, 2, 24, 128)] * 2
    scratch += [vm(2, 2, 32, 128)] * 2 + [vm(8, 2, 8, 128)] * 2
    scratch += [vm(4, 4, 2, 8, 128), vm(ROUNDS, 4, 4, 2, 8, 128), vm(2, *block)]
    scratch += [pltpu.SemaphoreType.DMA((10,)), pltpu.SemaphoreType.DMA((ROUNDS, 28)), pltpu.SemaphoreType.DMA((ROUNDS, 28))]
    out = jax.ShapeDtypeStruct((1, 8, 32, 256), F32)
    return pl.pallas_call(
        kernel,
        out_shape=(out, out),
        in_specs=[pl.BlockSpec(memory_space=pl.ANY)] * 3,
        out_specs=(pl.BlockSpec(memory_space=pl.ANY),) * 2,
        scratch_shapes=scratch,
        compiler_params=pltpu.CompilerParams(collective_id=0, has_side_effects=True, vmem_limit_bytes=48 * 1024 * 1024),
    )(u, v, s)


def solution(mesh):
    placed = (P("gx", "gy", None),) * 3
    return jax.shard_map(
        body,
        mesh=mesh,
        in_specs=placed,
        out_specs=(P("level", "gx", "gy", None),) * 2,
        check_vma=False,
    )
```

profile of v0, /device:TPU:1, one launch (start us, length us, event | category | flops | bytes accessed | tf_op | source)
XLA Modules:
  0.0 48.0 jit_solution(13752510446158968681)
XLA Ops:
  0.6 0.0 copy-start
  0.6 0.9 %copy-done = f32[8,32,256]{2,1,0:T(8,128)S(1)} copy-done((f32[8,32,256]{2,1,0:T(8,128)S(1)}, f32[8,32,256]{2,1,0:T(8,128)}, u32[]{:S(2)}) %copy-start) | copy-done | bytes 262168
  1.6 0.0 copy-start.1
  1.6 0.9 %copy-done.1 = f32[8,32,256]{2,1,0:T(8,128)S(1)} copy-done((f32[8,32,256]{2,1,0:T(8,128)S(1)}, f32[8,32,256]{2,1,0:T(8,128)}, u32[]{:S(2)}) %copy-start.1) | copy-done | bytes 262168
  2.5 0.0 copy-start.2
  2.5 0.9 %copy-done.2 = f32[8,32,256]{2,1,0:T(8,128)S(1)} copy-done((f32[8,32,256]{2,1,0:T(8,128)S(1)}, f32[8,32,256]{2,1,0:T(8,128)}, u32[]{:S(2)}) %copy-start.2) | copy-done | bytes 262168
  3.5 43.1 %shard_map.50 = (f32[1,8,32,256]{3,2,1,0:T(8,128)S(1)}, f32[1,8,32,256]{3,2,1,0:T(8,128)S(1)}) custom-call(f32[8,32,256]{2,1,0:T(8,128)S(1)} %copy-done, f32[8,32,256]{2,1,0:T(8,128)S(1)} %copy-done.1, f32[8,32,256]{2,1,0:T(8,128)S(1)} %copy-done.2), custom_call_target="tpu_custom_call" | custom-call | tf_op jit(solution)/shard_map/pallas_call | solution.py:384
  46.6 0.7 %copy.7 = f32[1,8,32,256]{3,2,1,0:T(8,128)} copy(f32[1,8,32,256]{3,2,1,0:T(8,128)S(1)} %get-tuple-element.4) | data formatting | bytes 524288
  47.3 0.7 %copy.8 = f32[1,8,32,256]{3,2,1,0:T(8,128)} copy(f32[1,8,32,256]{3,2,1,0:T(8,128)S(1)} %get-tuple-element.5) | data formatting | bytes 524288
Async XLA Ops:
  0.6 1.0 %copy-start = (f32[8,32,256]{2,1,0:T(8,128)S(1)}, f32[8,32,256]{2,1,0:T(8,128)}, u32[]{:S(2)}) copy-start(f32[8,32,256]{2,1,0:T(8,128)} %u_hbm.1) | copy-start | bytes 786436
  1.6 0.9 %copy-start.1 = (f32[8,32,256]{2,1,0:T(8,128)S(1)}, f32[8,32,256]{2,1,0:T(8,128)}, u32[]{:S(2)}) copy-start(f32[8,32,256]{2,1,0:T(8,128)} %v_hbm.1) | copy-start | bytes 786436
  2.5 0.9 %copy-start.2 = (f32[8,32,256]{2,1,0:T(8,128)S(1)}, f32[8,32,256]{2,1,0:T(8,128)}, u32[]{:S(2)}) copy-start(f32[8,32,256]{2,1,0:T(8,128)} %s_hbm.1) | copy-start | bytes 786436
where the time goes:
time: 48.2 us; the launch traced here: 48 us
  Pallas kernels  43.1 us (89%)
  local copies, waits for them, and re-layouts  4.25 us (9%)
  between operations  0.65 us (1%)
    pallas_call x1, Pallas kernels, body(): pl.pallas_call(kernel, out_shape=(out, out), in_specs=[pl.BlockSpec(memor...  43.1 us
    unnamed x8, local copies, waits for them, and re-layouts  4.25 us

commit v1 on v0

v1 whole, which is shorter than its diff:
```python
import functools

import jax
import jax.numpy as jnp
from jax import lax
from jax.experimental import pallas as pl
from jax.experimental.pallas import tpu as pltpu
from jax.sharding import PartitionSpec as P


H = 0.12
D = 0.05
W1 = 4.0 / 3.0
W2 = -1.0 / 12.0
ROUNDS = 3
MESH = pl.DeviceIdType.MESH
F32 = jnp.float32
XO, YO = 4, 8
OWN = slice(YO, YO + 32)
LO, HI = slice(0, 8), slice(40, 48)
RING = (-2, -1, 8, 9)
NEAREST = {0: (-1, -2), -1: (0, 1), 7: (8, 9), 8: (7, 6)}
NEXT = {1: -1, -2: 0, 6: 8, 9: 7}
DIAG = ((1, 1), (1, -1), (-1, 1), (-1, -1))


def rows(shape):
    return lax.broadcasted_iota(jnp.int32, shape, len(shape) - 2)


def turn(x, n):
    return pltpu.roll(x, n % 8, x.ndim - 2)


def from_below(c):
    r = rows(c.shape)
    return jnp.where(r == 0, W1 * turn(c, 1), 0.0) + jnp.where(r < 2, W2 * turn(c, 2), 0.0)


def from_above(c):
    r = rows(c.shape)
    return jnp.where(r == 7, W1 * turn(c, 7), 0.0) + jnp.where(r >= 6, W2 * turn(c, 6), 0.0)


def z_sums(a, b):
    lane = lax.broadcasted_iota(jnp.int32, a.shape, a.ndim - 1)
    ax = a.ndim - 1

    def shifted(n, mask):
        ra, rb = pltpu.roll(a, n % 128, ax), pltpu.roll(b, n % 128, ax)
        return jnp.where(mask, rb, ra), jnp.where(mask, ra, rb)

    l1, l2 = shifted(1, lane < 1), shifted(2, lane < 2)
    r1, r2 = shifted(127, lane >= 127), shifted(126, lane >= 126)
    return [(l1[i] + r1[i], l2[i] + r2[i]) for i in range(2)]


def lap(ref, p, lo, n, planes=None):
    at = (lambda q: q) if planes is None else (lambda q: pl.ds(q, planes))
    mid = [ref[at(p), f, lo : lo + n, :] for f in range(2)]
    zs = z_sums(*mid)
    out = []
    for f in range(2):
        near = zs[f][0] + ref[at(p - 1), f, lo : lo + n, :] + ref[at(p + 1), f, lo : lo + n, :]
        near = near + ref[at(p), f, lo - 1 : lo - 1 + n, :] + ref[at(p), f, lo + 1 : lo + 1 + n, :]
        far = zs[f][1] + ref[at(p - 2), f, lo : lo + n, :] + ref[at(p + 2), f, lo : lo + n, :]
        far = far + ref[at(p), f, lo - 2 : lo - 2 + n, :] + ref[at(p), f, lo + 2 : lo + 2 + n, :]
        out.append(W1 * near + (W2 * far - 7.5 * mid[f]))
    return out


def kernel(u_hbm, v_hbm, s_hbm, out_u, out_v, IU, I0, I1, I2, J1, J2, T0, T1, T2, TU, S, U, acc, A7, eW, eE, eS, eN, gW, gE,
           gS, gN, cs, cr, lsem, ssem, rsem):
    level = lax.axis_index("level")
    gx, gy = lax.axis_index("gx"), lax.axis_index("gy")
    nx, ny = lax.axis_size("gx"), lax.axis_size("gy")

    def peer(dx, dy):
        return (level, lax.rem(gx + dx + nx, nx), lax.rem(gy + dy + ny, ny))

    around = ((1, 0), (-1, 0), (0, 1), (0, -1)) + DIAG
    barrier = pltpu.get_barrier_semaphore()
    for d in around:
        pl.semaphore_signal(barrier, 1, device_id=peer(*d), device_id_type=MESH)

    loads = []
    for src, dst, off in ((v_hbm, I0, 2), (u_hbm, IU, 2), (s_hbm, S, XO)):
        for f in range(2):
            copy = pltpu.make_async_copy(
                src.at[:, :, 128 * f : 128 * f + 128], dst.at[off : off + 8, f, OWN, :], lsem.at[len(loads)]
            )
            copy.start()
            loads.append(copy)

    zero = jnp.zeros((2, 2, 48, 128), F32)
    for ref in (IU, I0, I1, I2, J1, J2):
        ref[0:2] = zero
        ref[10:12] = zero
        for sl in (LO, HI):
            ref[2:10, :, sl, :] = jnp.zeros((8, 2, 8, 128), F32)
    for ref in (eW, eE):
        ref[...] = jnp.zeros((6, 2, 48, 128), F32)
    for ref in (eS, eN):
        ref[...] = jnp.zeros((12, 2, 24, 128), F32)

    for copy in loads:
        copy.wait()

    def send(r, slot, src, dst, dx, dy):
        got = slot + 16 * (r % 2) if slot < 16 else slot + 16
        copy = pltpu.make_async_remote_copy(
            src_ref=src, dst_ref=dst, send_sem=ssem.at[slot], recv_sem=rsem.at[got],
            device_id=peer(dx, dy), device_id_type=MESH,
        )
        copy.start()
        return copy

    def send_x(r, slot, src, off, dst):
        return [
            send(r, slot, src.at[off + 6 : off + 8, :, OWN, :], dst.at[XO - 2 : XO, :, OWN, :], 1, 0),
            send(r, slot + 1, src.at[off : off + 2, :, OWN, :], dst.at[XO + 8 : XO + 10, :, OWN, :], -1, 0),
        ]

    def send_y(r, slot, src, off, dst):
        return [
            send(r, slot, src.at[off : off + 8, :, 32:40, :], dst.at[XO : XO + 8, :, LO, :], 0, 1),
            send(r, slot + 1, src.at[off : off + 8, :, 8:16, :], dst.at[XO : XO + 8, :, HI, :], 0, -1),
        ]

    def pack4(a, b, sy):
        r = rows(a.shape)
        return jnp.where(r >= 4 if sy > 0 else r < 4, b, turn(a, 4))

    def pack2(items, sy):
        r = rows(items[0].shape)
        out = items[0]
        for i in range(1, 4):
            first = ((6 if sy > 0 else 0) + 2 * i) % 8
            out = jnp.where((r == first) | (r == first + 1), turn(items[i], 2 * i), out)
        return out

    def corner(sx, sy):
        near = (6, 7) if sx > 0 else (0, 1)
        far = (4, 5) if sx > 0 else (2, 3)
        return near, far, (slice(32, 40) if sy > 0 else slice(8, 16))

    def corner_in(sx, sy):
        near = (XO - 2, XO - 1) if sx > 0 else (XO + 8, XO + 9)
        far = (XO - 4, XO - 3) if sx > 0 else (XO + 10, XO + 11)
        return near, far, (LO if sy > 0 else HI)

    def start(p, c):
        for f, value in enumerate(lap(IU, p + 2, YO, 32)):
            U[p, f] = value
            acc[p, f] = IU[p + 2, f, OWN, :]
        return c

    def alone1(p, c):
        for f, value in enumerate(lap(I0, p + 2, YO, 32)):
            u = U[p, f]
            new = I0[p + 2, f, OWN, :] + H * (S[p + XO, f, OWN, :] * u + D * value)
            I1[p + 2, f, OWN, :] = new
            J1[p + 2, f, OWN, :] = new
            U[p, f] = u + H * value
        return c

    def alone2(p, c):
        for f, value in enumerate(lap(I1, p + 2, YO, 32)):
            I2[p + 2, f, OWN, :] = I1[p + 2, f, OWN, :] + H * (S[p + XO, f, OWN, :] * U[p, f] + D * value)
        return c

    def cross_x(own, ring, x, sl):
        at = (lambda q: own[q + 2, :, OWN, :]) if sl is OWN and x in RING else (lambda q: ring[q + XO, :, sl, :])
        if x in NEAREST:
            a, b = NEAREST[x]
            return W1 * at(a) + W2 * at(b)
        return W2 * at(NEXT[x])

    ends = ((slice(8, 16), from_below, LO), (slice(32, 40), from_above, HI))

    def fix_ends(ring, p, put):
        for sl, cross, g in ends:
            put(p, sl, lambda ref: cross(ref[p + XO, :, g, :]))

    def fix_faces(ring, put):
        for x in (0, 1, 6, 7):
            put(x, OWN, lambda ref: cross_x(None, ref, x, OWN))
            fix_ends(ring, x, put)

    def fix_inner(ring, put):
        def step(p, c):
            fix_ends(ring, p, put)
            return c

        lax.fori_loop(2, 6, step, 0)

    def off(sl):
        return slice(sl.start - YO, sl.stop - YO)

    def pack(i, first):
        sx, sy = DIAG[i]
        near, far, sl = corner(sx, sy)
        cs[i, 0] = pack4(*[I0[q + 2, :, sl, :] for q in near], sy)
        cs[i, 1] = pack2([I0[q + 2, :, sl, :] for q in far] + [I1[q + 2, :, sl, :] for q in near], sy)
        if first:
            cs[i, 2] = pack4(*[IU[q + 2, :, sl, :] for q in near], sy)
            cs[i, 3] = pack2([IU[q + 2, :, sl, :] for q in far] + [S[q + XO, :, sl, :] for q in near], sy)

    def send_diag(r, n):
        return [send(r, 12 + i, cs.at[i, 0:n], cr.at[r, i, 0:n], *DIAG[i]) for i in range(4)]

    def faces_first(step):
        lax.fori_loop(0, 4, lambda i, c: step(i + 4 * (i // 2), c), 0)

    def inner(step):
        lax.fori_loop(2, 6, step, 0)

    x0 = y0 = None
    for r in range(ROUNDS):
        first, last = r == 0, r == ROUNDS - 1
        t0, t1, t2 = T0.at[r], T1.at[r], T2.at[r]
        extra = []
        if first:
            pl.semaphore_wait(barrier, len(around))
            x0 = send_x(r, 0, I0, 2, t0)
            y0 = send_y(r, 2, I0, 2, t0)
            extra = send_x(r, 16, IU, 2, TU) + send_y(r, 18, IU, 2, TU)
            extra += send_x(r, 20, S, XO, S) + send_y(r, 22, S, XO, S)
            for i, sl in enumerate((slice(8, 16), slice(32, 40))):
                extra.append(send(r, 24 + 2 * i, S.at[XO + 4 : XO + 6, :, sl, :], S.at[XO - 4 : XO - 2, :, sl, :], 1, 0))
                extra.append(send(r, 25 + 2 * i, S.at[XO + 2 : XO + 4, :, sl, :], S.at[XO + 10 : XO + 12, :, sl, :], -1, 0))
            lax.fori_loop(0, 8, start, 0)
        faces_first(alone1)
        x1 = send_x(r, 4, I1, 2, t1)
        for i in range(4):
            pack(i, first)
        diag = send_diag(r, 4 if first else 2)
        inner(alone1)
        y1 = send_y(r, 6, I1, 2, t1)
        faces_first(alone2)
        x2 = send_x(r, 8, I2, 2, t2)
        inner(alone2)
        y2 = send_y(r, 10, I2, 2, t2)

        for copy in y0 + x0 + extra:
            copy.wait()

        def put1(p, sl, cross):
            xv = cross(t0)
            add, grow = H * D * xv, H * xv
            if first:
                xu = cross(TU)
                add, grow = add + H * (S[p + XO, :, sl, :] * xu), grow + xu
            J1[p + 2, :, sl, :] = J1[p + 2, :, sl, :] + add
            U[p, :, off(sl), :] = U[p, :, off(sl), :] + grow

        fix_faces(t0, put1)
        fix_inner(t0, put1)

        def own2(p, c):
            for f, value in enumerate(lap(J1, p + 2, YO, 32)):
                u = U[p, f]
                a = S[p + XO, f, OWN, :] * u + D * value
                J2[p + 2, f, OWN, :] = J1[p + 2, f, OWN, :] + H * a
                if last:
                    A7[p, f] = a
                U[p, f] = u + H * value
            return c

        lax.fori_loop(0, 8, own2, 0)

        for copy in diag:
            copy.wait()
        for i, (sx, sy) in enumerate(DIAG):
            near, far, sl = corner_in(sx, sy)
            for k, ref in ((0, t0), (2, TU))[: 2 if first else 1]:
                ref[near[1], :, sl, :] = cr[r, i, k]
                ref[near[0], :, sl, :] = turn(cr[r, i, k], 4)
                ref[far[0], :, sl, :] = cr[r, i, k + 1]
                ref[far[1], :, sl, :] = turn(cr[r, i, k + 1], 6)
            for k, ref in ((1, t1), (3, S))[: 2 if first else 1]:
                ref[near[0], :, sl, :] = turn(cr[r, i, k], 4)
                ref[near[1], :, sl, :] = turn(cr[r, i, k], 2)

        def both(cross, *where):
            xv = cross(I0, t0)
            e, g = H * D * xv, H * xv
            if first:
                xu = cross(IU, TU)
                e, g = e + H * (S[where] * xu), g + xu
            return e, g

        every = slice(None)
        for e_ref, g_ref, near, far, base in ((eW, gW, (-2, -1), (-4, -3), -4), (eE, gE, (8, 9), (10, 11), 6)):
            for x in near:
                e, g = both(lambda own, ring: cross_x(own, ring, x, OWN), x + XO, every, OWN)
                e_ref[x - base, :, OWN, :] = e
                g_ref[x - near[0]] = g
            for x in near + far:
                for sl, cross, g_sl in ends:
                    e, g = both(lambda own, ring: cross(ring[x + XO, :, g_sl, :]), x + XO, every, sl)
                    if x in near:
                        e_ref[x - base, :, sl, :] = e_ref[x - base, :, sl, :] + e
                        g_ref[x - near[0], :, off(sl), :] = g_ref[x - near[0], :, off(sl), :] + g
                    else:
                        e_ref[x - base, :, sl, :] = e
        sides = ((eS, gS, LO, from_above, slice(8, 16)), (eN, gN, HI, from_below, slice(32, 40)))
        mid = slice(XO, XO + 8)
        for e_ref, g_ref, sl, cross, o_sl in sides:
            e, g = both(lambda own, ring: cross(own[2:10, :, o_sl, :]), mid, every, sl)
            e_ref[2:10, :, 8:16, :] = e
            g_ref[...] = g
            for x in (0, 1, 6, 7):
                e, g = both(lambda own, ring: cross_x(own, ring, x, sl), x + XO, every, sl)
                e_ref[x + 2, :, 8:16, :] = e_ref[x + 2, :, 8:16, :] + e
                g_ref[x] = g_ref[x] + g
            for x in RING:
                e, g = both(
                    lambda own, ring: cross_x(own, ring, x, sl) + cross(ring[x + XO, :, o_sl, :]), x + XO, every, sl
                )
                t1[x + XO, :, sl, :] = t1[x + XO, :, sl, :] + e

        for e_ref, g_ref, near, base in ((eW, gW, (-2, -1), -4), (eE, gE, (8, 9), 6)):
            for x in near:
                value = lap(e_ref, x - base, YO, 32)
                cx = cross_x(J1, t1, x, OWN)
                for f in range(2):
                    full = value[f] + cx[f]
                    low = full[0:8] + from_below(t1[x + XO, f, LO, :])
                    high = full[24:32] + from_above(t1[x + XO, f, HI, :])
                    full = jnp.concatenate([low, full[8:24], high], axis=0)
                    e = e_ref[x - base, f, OWN, :] + H * (S[x + XO, f, OWN, :] * g_ref[x - near[0], f] + D * full)
                    g_ref[x - near[0], f] = e
        for e_ref, g_ref, sl, cross, o_sl in sides:
            value = lap(e_ref, 2, 8, 8, planes=8)
            for f in range(2):
                full = value[f] + cross(J1[2:10, f, o_sl, :])
                e = e_ref[2:10, f, 8:16, :] + H * (S[mid, f, sl, :] * g_ref[:, f] + D * full)
                g_ref[:, f] = e
            for x in (0, 1, 6, 7):
                g_ref[x] = g_ref[x] + H * D * cross_x(None, t1, x, sl)

        for copy in y1 + x1:
            copy.wait()
        for e_ref, x, k in ((eW, XO - 2, 2), (eE, XO + 8, 2)):
            t1[x : x + 2, :, OWN, :] = t1[x : x + 2, :, OWN, :] + e_ref[k : k + 2, :, OWN, :]
        for e_ref, g_ref, sl, cross, o_sl in sides:
            t1[mid, :, sl, :] = t1[mid, :, sl, :] + e_ref[2:10, :, 8:16, :]

        def put2(p, sl, cross):
            xv = cross(t1)
            J2[p + 2, :, sl, :] = J2[p + 2, :, sl, :] + H * D * xv
            U[p, :, off(sl), :] = U[p, :, off(sl), :] + H * xv
            if last:
                A7[p, :, off(sl), :] = A7[p, :, off(sl), :] + D * xv

        fix_faces(t1, put2)
        fix_inner(t1, put2)

        raised = level == 1

        def own3(p, c):
            for f, value in enumerate(lap(J2, p + 2, YO, 32)):
                u, v8, v7 = U[p, f], J2[p + 2, f, OWN, :], J1[p + 2, f, OWN, :]
                a8 = S[p + XO, f, OWN, :] * u + D * value
                if last:
                    u8 = acc[p, f] + H * (I0[p + 2, f, OWN, :] + v7)
                    lanes = slice(128 * f, 128 * f + 128)
                    out_u[0, p, :, lanes] = jnp.where(raised, u8 + 4 * H * (v8 - v7), u8)
                    out_v[0, p, :, lanes] = jnp.where(raised, v8 + 4 * H * (a8 - A7[p, f]), v8)
                else:
                    acc[p, f] = acc[p, f] + H * (I0[p + 2, f, OWN, :] + v7 + v8)
                    I0[p + 2, f, OWN, :] = v8 + H * a8
                    U[p, f] = u + H * value
            return c

        lax.fori_loop(0, 8, own3, 0)

        for copy in y2 + x2:
            copy.wait()
        for g_ref, x in ((gW, XO - 2), (gE, XO + 8)):
            t2[x : x + 2, :, OWN, :] = t2[x : x + 2, :, OWN, :] + g_ref[...]
        for e_ref, g_ref, sl, cross, o_sl in sides:
            t2[mid, :, sl, :] = t2[mid, :, sl, :] + g_ref[...]

        def put3(p, sl, cross):
            xv = cross(t2)
            if last:
                for f in range(2):
                    lanes = slice(128 * f, 128 * f + 128)
                    old = out_v[0, p, off(sl), lanes]
                    out_v[0, p, off(sl), lanes] = jnp.where(raised, old + 4 * H * D * xv[f], old)
            else:
                I0[p + 2, :, sl, :] = I0[p + 2, :, sl, :] + H * D * xv
                U[p, :, off(sl), :] = U[p, :, off(sl), :] + H * xv

        fix_faces(t2, put3)
        if not last:
            x0 = send_x(r + 1, 0, I0, 2, T0.at[r + 1])
        fix_inner(t2, put3)
        if not last:
            y0 = send_y(r + 1, 2, I0, 2, T0.at[r + 1])


def body(u, v, s):
    ext, alone, block = (16, 2, 48, 128), (12, 2, 48, 128), (8, 2, 32, 128)
    vm = lambda *shape: pltpu.VMEM(shape, F32)
    scratch = [vm(*alone)] * 6 + [vm(ROUNDS, *ext)] * 3 + [vm(*ext)] * 2 + [vm(*block)] * 3
    scratch += [vm(6, 2, 48, 128)] * 2 + [vm(12, 2, 24, 128)] * 2
    scratch += [vm(2, 2, 32, 128)] * 2 + [vm(8, 2, 8, 128)] * 2
    scratch += [vm(4, 4, 2, 8, 128), vm(ROUNDS, 4, 4, 2, 8, 128)]
    scratch += [pltpu.SemaphoreType.DMA((6,)), pltpu.SemaphoreType.DMA((28,)), pltpu.SemaphoreType.DMA((44,))]
    out = jax.ShapeDtypeStruct((1, 8, 32, 256), F32)
    return pl.pallas_call(
        kernel,
        out_shape=(out, out),
        in_specs=[pl.BlockSpec(memory_space=pltpu.HBM)] * 3,
        out_specs=(pl.BlockSpec(memory_space=pltpu.VMEM),) * 2,
        scratch_shapes=scratch,
        compiler_params=pltpu.CompilerParams(collective_id=0, has_side_effects=True, vmem_limit_bytes=48 * 1024 * 1024),
    )(*[pltpu.with_memory_space_constraint(x, pltpu.HBM) for x in (u, v, s)])


def solution(mesh):
    placed = (P("gx", "gy", None),) * 3
    return jax.shard_map(
        body,
        mesh=mesh,
        in_specs=placed,
        out_specs=(P("level", "gx", "gy", None),) * 2,
        check_vma=False,
    )
```

time: 48.2 us -> 41.8 us (0.87)
  Pallas kernels: 43.1 us -> 39.6 us
  local copies, waits for them, and re-layouts: 4.25 us -> 1.41 us
    pallas_call x1, Pallas kernels: 43.1 us -> 39.6 us  [body(): pl.pallas_call(kernel, out_shape=(out, out), in_specs=[pl.BlockSpec(memor...]
    unnamed x8 -> x2, local copies, waits for them, and re-layouts: 4.25 us -> 1.41 us
where the time goes in v1:
time: 41.8 us; the launch traced here: 41.7 us
  Pallas kernels  39.6 us (95%)
  local copies, waits for them, and re-layouts  1.41 us (3%)
  between operations  0.64 us (2%)
    pallas_call x1, Pallas kernels, body(): pl.pallas_call(kernel, out_shape=(out, out), in_specs=[pl.BlockSpec(memor...  39.6 us
    unnamed x2, local copies, waits for them, and re-layouts  1.41 us

profile of v1, /device:TPU:1, one launch (start us, length us, event | category | flops | bytes accessed | tf_op | source)
XLA Modules:
  0.0 41.7 jit_solution(12664133133021743926)
XLA Ops:
  0.6 39.6 %shard_map.50 = (f32[1,8,32,256]{3,2,1,0:T(8,128)S(1)}, f32[1,8,32,256]{3,2,1,0:T(8,128)S(1)}) custom-call(f32[8,32,256]{2,1,0:T(8,128)} %u_hbm.1, f32[8,32,256]{2,1,0:T(8,128)} %v_hbm.1, f32[8,32,256]{2,1,0:T(8,128)} %s_hbm.1), custom_call_target="tpu_custom_call" | custom-call | tf_op jit(solution)/shard_map/pallas_call | solution.py:414
  40.3 0.7 %copy.7 = f32[1,8,32,256]{3,2,1,0:T(8,128)} copy(f32[1,8,32,256]{3,2,1,0:T(8,128)S(1)} %get-tuple-element.4) | data formatting | bytes 524288
  41.0 0.7 %copy.8 = f32[1,8,32,256]{3,2,1,0:T(8,128)} copy(f32[1,8,32,256]{3,2,1,0:T(8,128)S(1)} %get-tuple-element.5) | data formatting | bytes 524288

commit v2 on v1

--- a/solution.py
+++ b/solution.py
@@ -70,7 +70,7 @@
 
 
 def kernel(u_hbm, v_hbm, s_hbm, out_u, out_v, IU, I0, I1, I2, J1, J2, T0, T1, T2, TU, S, U, acc, A7, eW, eE, eS, eN, gW, gE,
-           gS, gN, cs, cr, lsem, ssem, rsem):
+           gS, gN, cs, cr, fs, fr, lsem, ssem, rsem):
     level = lax.axis_index("level")
     gx, gy = lax.axis_index("gx"), lax.axis_index("gy")
     nx, ny = lax.axis_size("gx"), lax.axis_size("gy")
@@ -107,7 +107,7 @@
         copy.wait()
 
     def send(r, slot, src, dst, dx, dy):
-        got = slot + 16 * (r % 2) if slot < 16 else slot + 16
+        got = slot + 20 * (r % 2) if slot < 20 else slot + 20
         copy = pltpu.make_async_remote_copy(
             src_ref=src, dst_ref=dst, send_sem=ssem.at[slot], recv_sem=rsem.at[got],
             device_id=peer(dx, dy), device_id_type=MESH,
@@ -197,17 +197,32 @@
     def off(sl):
         return slice(sl.start - YO, sl.stop - YO)
 
+    def halves(ref, planes, shift, sl):
+        return [ref[q + shift, f, sl, :] for f in range(2) for q in planes]
+
     def pack(i, first):
         sx, sy = DIAG[i]
         near, far, sl = corner(sx, sy)
-        cs[i, 0] = pack4(*[I0[q + 2, :, sl, :] for q in near], sy)
-        cs[i, 1] = pack2([I0[q + 2, :, sl, :] for q in far] + [I1[q + 2, :, sl, :] for q in near], sy)
+        for k, ref in ((0, I0), (3, IU))[: 2 if first else 1]:
+            for f in range(2):
+                cs[i, k + f] = pack4(*[ref[q + 2, f, sl, :] for q in near], sy)
+            cs[i, k + 2] = pack2(halves(ref, far, 2, sl), sy)
         if first:
-            cs[i, 2] = pack4(*[IU[q + 2, :, sl, :] for q in near], sy)
-            cs[i, 3] = pack2([IU[q + 2, :, sl, :] for q in far] + [S[q + XO, :, sl, :] for q in near], sy)
-
-    def send_diag(r, n):
+            cs[i, 6] = pack2(halves(S, near, XO, sl), sy)
+
+    def send_corners(r, n):
         return [send(r, 12 + i, cs.at[i, 0:n], cr.at[r, i, 0:n], *DIAG[i]) for i in range(4)]
+
+    def send_corners1(r):
+        copies = []
+        for i, (sx, sy) in enumerate(DIAG):
+            near, far, sl = corner(sx, sy)
+            cs[i, 7] = pack2(halves(I1, near, 2, sl), sy)
+            copies.append(send(r, 16 + i, cs.at[i, 7:8], cr.at[r, i, 7:8], sx, sy))
+        return copies
+
+    def unpack2(tile):
+        return [[turn(tile, -2 * (q + 2 * f)) for f in range(2)] for q in range(2)]
 
     def faces_first(step):
         lax.fori_loop(0, 4, lambda i, c: step(i + 4 * (i // 2), c), 0)
@@ -221,20 +236,24 @@
         t0, t1, t2 = T0.at[r], T1.at[r], T2.at[r]
         extra = []
         if first:
+            for k, planes in enumerate(((4, 5), (2, 3))):
+                for f in range(2):
+                    a, b, c, d = [S[q + XO, f, sl, :] for q in planes for sl in (slice(8, 16), slice(32, 40))]
+                    i = rows(a.shape)
+                    fs[k, f] = jnp.where(i < 2, a, jnp.where(i >= 6, b, jnp.where(i < 4, turn(c, 2), turn(d, 6))))
+            for i in range(4):
+                pack(i, True)
             pl.semaphore_wait(barrier, len(around))
             x0 = send_x(r, 0, I0, 2, t0)
             y0 = send_y(r, 2, I0, 2, t0)
-            extra = send_x(r, 16, IU, 2, TU) + send_y(r, 18, IU, 2, TU)
-            extra += send_x(r, 20, S, XO, S) + send_y(r, 22, S, XO, S)
-            for i, sl in enumerate((slice(8, 16), slice(32, 40))):
-                extra.append(send(r, 24 + 2 * i, S.at[XO + 4 : XO + 6, :, sl, :], S.at[XO - 4 : XO - 2, :, sl, :], 1, 0))
-                extra.append(send(r, 25 + 2 * i, S.at[XO + 2 : XO + 4, :, sl, :], S.at[XO + 10 : XO + 12, :, sl, :], -1, 0))
+            extra = send_x(r, 20, IU, 2, TU) + send_y(r, 22, IU, 2, TU)
+            diag = send_corners(r, 7)
+            extra += send_x(r, 24, S, XO, S) + send_y(r, 26, S, XO, S)
+            extra += [send(r, 28, fs.at[0], fr.at[0], 1, 0), send(r, 29, fs.at[1], fr.at[1], -1, 0)]
             lax.fori_loop(0, 8, start, 0)
         faces_first(alone1)
         x1 = send_x(r, 4, I1, 2, t1)
-        for i in range(4):
-            pack(i, first)
-        diag = send_diag(r, 4 if first else 2)
+        diag1 = send_corners1(r)
         inner(alone1)
         y1 = send_y(r, 6, I1, 2, t1)
         faces_first(alone2)
@@ -273,14 +292,25 @@
             copy.wait()
         for i, (sx, sy) in enumerate(DIAG):
             near, far, sl = corner_in(sx, sy)
-            for k, ref in ((0, t0), (2, TU))[: 2 if first else 1]:
-                ref[near[1], :, sl, :] = cr[r, i, k]
-                ref[near[0], :, sl, :] = turn(cr[r, i, k], 4)
-                ref[far[0], :, sl, :] = cr[r, i, k + 1]
-                ref[far[1], :, sl, :] = turn(cr[r, i, k + 1], 6)
-            for k, ref in ((1, t1), (3, S))[: 2 if first else 1]:
-                ref[near[0], :, sl, :] = turn(cr[r, i, k], 4)
-                ref[near[1], :, sl, :] = turn(cr[r, i, k], 2)
+            for k, ref in ((0, t0), (3, TU))[: 2 if first else 1]:
+                ends2 = unpack2(cr[r, i, k + 2])
+                for f in range(2):
+                    ref[near[1], f, sl, :] = cr[r, i, k + f]
+                    ref[near[0], f, sl, :] = turn(cr[r, i, k + f], 4)
+                    ref[far[0], f, sl, :] = ends2[0][f]
+                    ref[far[1], f, sl, :] = ends2[1][f]
+            if first:
+                ends2 = unpack2(cr[r, i, 6])
+                for q in range(2):
+                    for f in range(2):
+                        S[near[q], f, sl, :] = ends2[q][f]
+        if first:
+            for k, x in enumerate((XO - 4, XO + 10)):
+                for f in range(2):
+                    S[x, f, 8:16, :] = fr[k, f]
+                    S[x, f, 32:40, :] = fr[k, f]
+                    S[x + 1, f, 8:16, :] = turn(fr[k, f], 6)
+                    S[x + 1, f, 32:40, :] = turn(fr[k, f], 2)
 
         def both(cross, *where):
             xv = cross(I0, t0)
@@ -318,7 +348,7 @@
                 e, g = both(
                     lambda own, ring: cross_x(own, ring, x, sl) + cross(ring[x + XO, :, o_sl, :]), x + XO, every, sl
                 )
-                t1[x + XO, :, sl, :] = t1[x + XO, :, sl, :] + e
+                t1[x + XO, :, sl, :] = e
 
         for e_ref, g_ref, near, base in ((eW, gW, (-2, -1), -4), (eE, gE, (8, 9), 6)):
             for x in near:
@@ -326,9 +356,6 @@
                 cx = cross_x(J1, t1, x, OWN)
                 for f in range(2):
                     full = value[f] + cx[f]
-                    low = full[0:8] + from_below(t1[x + XO, f, LO, :])
-                    high = full[24:32] + from_above(t1[x + XO, f, HI, :])
-                    full = jnp.concatenate([low, full[8:24], high], axis=0)
                     e = e_ref[x - base, f, OWN, :] + H * (S[x + XO, f, OWN, :] * g_ref[x - near[0], f] + D * full)
                     g_ref[x - near[0], f] = e
         for e_ref, g_ref, sl, cross, o_sl in sides:
@@ -337,8 +364,6 @@
                 full = value[f] + cross(J1[2:10, f, o_sl, :])
                 e = e_ref[2:10, f, 8:16, :] + H * (S[mid, f, sl, :] * g_ref[:, f] + D * full)
                 g_ref[:, f] = e
-            for x in (0, 1, 6, 7):
-                g_ref[x] = g_ref[x] + H * D * cross_x(None, t1, x, sl)
 
         for copy in y1 + x1:
             copy.wait()
@@ -376,6 +401,23 @@
 
         lax.fori_loop(0, 8, own3, 0)
 
+        for copy in diag1:
+            copy.wait()
+        for i, (sx, sy) in enumerate(DIAG):
+            near, far, sl = corner_in(sx, sy)
+            ends2 = unpack2(cr[r, i, 7])
+            for q in range(2):
+                for f in range(2):
+                    t1[near[q], f, sl, :] = t1[near[q], f, sl, :] + ends2[q][f]
+        for g_ref, near in ((gW, (-2, -1)), (gE, (8, 9))):
+            for x in near:
+                for sl, cross, g_sl in ends:
+                    q = x - near[0]
+                    g_ref[q, :, off(sl), :] = g_ref[q, :, off(sl), :] + H * D * cross(t1[x + XO, :, g_sl, :])
+        for e_ref, g_ref, sl, cross, o_sl in sides:
+            for x in (0, 1, 6, 7):
+                g_ref[x] = g_ref[x] + H * D * cross_x(None, t1, x, sl)
+
         for copy in y2 + x2:
             copy.wait()
         for g_ref, x in ((gW, XO - 2), (gE, XO + 8)):
@@ -399,6 +441,9 @@
             x0 = send_x(r + 1, 0, I0, 2, T0.at[r + 1])
         fix_inner(t2, put3)
         if not last:
+            for i in range(4):
+                pack(i, False)
+            diag = send_corners(r + 1, 3)
             y0 = send_y(r + 1, 2, I0, 2, T0.at[r + 1])
 
 
@@ -408,8 +453,8 @@
     scratch = [vm(*alone)] * 6 + [vm(ROUNDS, *ext)] * 3 + [vm(*ext)] * 2 + [vm(*block)] * 3
     scratch += [vm(6, 2, 48, 128)] * 2 + [vm(12, 2, 24, 128)] * 2
     scratch += [vm(2, 2, 32, 128)] * 2 + [vm(8, 2, 8, 128)] * 2
-    scratch += [vm(4, 4, 2, 8, 128), vm(ROUNDS, 4, 4, 2, 8, 128)]
-    scratch += [pltpu.SemaphoreType.DMA((6,)), pltpu.SemaphoreType.DMA((28,)), pltpu.SemaphoreType.DMA((44,))]
+    scratch += [vm(4, 8, 8, 128), vm(ROUNDS, 4, 8, 8, 128), vm(2, 2, 8, 128), vm(2, 2, 8, 128)]
+    scratch += [pltpu.SemaphoreType.DMA((6,)), pltpu.SemaphoreType.DMA((30,)), pltpu.SemaphoreType.DMA((50,))]
     out = jax.ShapeDtypeStruct((1, 8, 32, 256), F32)
     return pl.pallas_call(
         kernel,

time: 41.8 us -> 38.8 us (0.928)
  Pallas kernels: 39.6 us -> 36.7 us
    pallas_call x1, Pallas kernels: 39.6 us -> 36.7 us  [body(): pl.pallas_call(kernel, out_shape=(out, out), in_specs=[pl.BlockSpec(memor...]
where the time goes in v2:
time: 38.8 us; the launch traced here: 38.7 us
  Pallas kernels  36.7 us (95%)
  local copies, waits for them, and re-layouts  1.41 us (4%)
  between operations  0.64 us (2%)
    pallas_call x1, Pallas kernels, body(): pl.pallas_call(kernel, out_shape=(out, out), in_specs=[pl.BlockSpec(memor...  36.7 us
    unnamed x2, local copies, waits for them, and re-layouts  1.41 us

profile of v2, /device:TPU:1, one launch (start us, length us, event | category | flops | bytes accessed | tf_op | source)
XLA Modules:
  0.0 38.7 jit_solution(16195680195536610289)
XLA Ops:
  0.6 36.7 %shard_map.50 = (f32[1,8,32,256]{3,2,1,0:T(8,128)S(1)}, f32[1,8,32,256]{3,2,1,0:T(8,128)S(1)}) custom-call(f32[8,32,256]{2,1,0:T(8,128)} %u_hbm.1, f32[8,32,256]{2,1,0:T(8,128)} %v_hbm.1, f32[8,32,256]{2,1,0:T(8,128)} %s_hbm.1), custom_call_target="tpu_custom_call" | custom-call | tf_op jit(solution)/shard_map/pallas_call | solution.py:459
  37.3 0.7 %copy.7 = f32[1,8,32,256]{3,2,1,0:T(8,128)} copy(f32[1,8,32,256]{3,2,1,0:T(8,128)S(1)} %get-tuple-element.4) | data formatting | bytes 524288
  38.0 0.7 %copy.8 = f32[1,8,32,256]{3,2,1,0:T(8,128)} copy(f32[1,8,32,256]{3,2,1,0:T(8,128)S(1)} %get-tuple-element.5) | data formatting | bytes 524288

commit v3 on v2

--- a/solution.py
+++ b/solution.py
@@ -69,8 +69,20 @@
     return out
 
 
+def lap_z(ref, p, zs):
+    out = []
+    for f in range(2):
+        mid = ref[p, f, OWN, :]
+        near = ref[p - 1, f, OWN, :] + ref[p + 1, f, OWN, :]
+        near = near + (ref[p, f, YO - 1 : YO + 31, :] + ref[p, f, YO + 1 : YO + 33, :])
+        far = ref[p - 2, f, OWN, :] + ref[p + 2, f, OWN, :]
+        far = far + (ref[p, f, YO - 2 : YO + 30, :] + ref[p, f, YO + 2 : YO + 34, :])
+        out.append(W1 * near + (W2 * far - 5.0 * mid) + (1.0 / 12.0) * zs[f])
+    return out
+
+
 def kernel(u_hbm, v_hbm, s_hbm, out_u, out_v, IU, I0, I1, I2, J1, J2, T0, T1, T2, TU, S, U, acc, A7, eW, eE, eS, eN, gW, gE,
-           gS, gN, cs, cr, fs, fr, lsem, ssem, rsem):
+           gS, gN, cs, cr, fs, fr, Z, band, lsem, ssem, rsem):
     level = lax.axis_index("level")
     gx, gy = lax.axis_index("gx"), lax.axis_index("gy")
     nx, ny = lax.axis_size("gx"), lax.axis_size("gy")
@@ -103,8 +115,29 @@
     for ref in (eS, eN):
         ref[...] = jnp.zeros((12, 2, 24, 128), F32)
 
+    gap = lax.broadcasted_iota(jnp.int32, (256, 256), 0) - lax.broadcasted_iota(jnp.int32, (256, 256), 1)
+    gap = jnp.abs(gap)
+    gap = jnp.minimum(gap, 256 - gap)
+    weight = jnp.where(gap == 0, -30.0, jnp.where(gap == 1, 16.0, jnp.where(gap == 2, -1.0, 0.0)))
+    band[...] = weight.astype(jnp.bfloat16)
+
     for copy in loads:
         copy.wait()
+
+    def along_z(ref, planes):
+        rest = jnp.concatenate(
+            [jnp.concatenate([ref[p + 2, f, OWN, :] for f in range(2)], axis=1) for p in planes], axis=0
+        )
+        parts = []
+        for _ in range(3):
+            parts.append(rest.astype(jnp.bfloat16))
+            rest = rest - parts[-1].astype(F32)
+        n = 32 * len(planes)
+        out = jnp.dot(jnp.concatenate(parts, axis=0), band[...], preferred_element_type=F32)
+        out = out[0:n] + (out[n : 2 * n] + out[2 * n : 3 * n])
+        for i, p in enumerate(planes):
+            for f in range(2):
+                Z[p, f] = out[32 * i : 32 * i + 32, 128 * f : 128 * f + 128]
 
     def send(r, slot, src, dst, dx, dy):
         got = slot + 20 * (r % 2) if slot < 20 else slot + 20
@@ -150,13 +183,13 @@
         return near, far, (LO if sy > 0 else HI)
 
     def start(p, c):
-        for f, value in enumerate(lap(IU, p + 2, YO, 32)):
+        for f, value in enumerate(lap_z(IU, p + 2, Z[p])):
             U[p, f] = value
             acc[p, f] = IU[p + 2, f, OWN, :]
         return c
 
     def alone1(p, c):
-        for f, value in enumerate(lap(I0, p + 2, YO, 32)):
+        for f, value in enumerate(lap_z(I0, p + 2, Z[p])):
             u = U[p, f]
             new = I0[p + 2, f, OWN, :] + H * (S[p + XO, f, OWN, :] * u + D * value)
             I1[p + 2, f, OWN, :] = new
@@ -165,7 +198,7 @@
         return c
 
     def alone2(p, c):
-        for f, value in enumerate(lap(I1, p + 2, YO, 32)):
+        for f, value in enumerate(lap_z(I1, p + 2, Z[p])):
             I2[p + 2, f, OWN, :] = I1[p + 2, f, OWN, :] + H * (S[p + XO, f, OWN, :] * U[p, f] + D * value)
         return c
 
@@ -192,7 +225,7 @@
             fix_ends(ring, p, put)
             return c
 
-        lax.fori_loop(2, 6, step, 0)
+        lax.fori_loop(2, 6, step, 0, unroll=4)
 
     def off(sl):
         return slice(sl.start - YO, sl.stop - YO)
@@ -224,11 +257,13 @@
     def unpack2(tile):
         return [[turn(tile, -2 * (q + 2 * f)) for f in range(2)] for q in range(2)]
 
-    def faces_first(step):
-        lax.fori_loop(0, 4, lambda i, c: step(i + 4 * (i // 2), c), 0)
-
-    def inner(step):
-        lax.fori_loop(2, 6, step, 0)
+    def faces_first(step, ref):
+        along_z(ref, (0, 1, 6, 7))
+        lax.fori_loop(0, 4, lambda i, c: step(i + 4 * (i // 2), c), 0, unroll=4)
+
+    def inner(step, ref):
+        along_z(ref, (2, 3, 4, 5))
+        lax.fori_loop(2, 6, step, 0, unroll=4)
 
     x0 = y0 = None
     for r in range(ROUNDS):
@@ -250,15 +285,16 @@
             diag = send_corners(r, 7)
             extra += send_x(r, 24, S, XO, S) + send_y(r, 26, S, XO, S)
             extra += [send(r, 28, fs.at[0], fr.at[0], 1, 0), send(r, 29, fs.at[1], fr.at[1], -1, 0)]
-            lax.fori_loop(0, 8, start, 0)
-        faces_first(alone1)
+            faces_first(start, IU)
+            inner(start, IU)
+        faces_first(alone1, I0)
+        diag1 = send_corners1(r)
         x1 = send_x(r, 4, I1, 2, t1)
-        diag1 = send_corners1(r)
-        inner(alone1)
+        inner(alone1, I0)
         y1 = send_y(r, 6, I1, 2, t1)
-        faces_first(alone2)
+        faces_first(alone2, I1)
         x2 = send_x(r, 8, I2, 2, t2)
-        inner(alone2)
+        inner(alone2, I1)
         y2 = send_y(r, 10, I2, 2, t2)
 
         for copy in y0 + x0 + extra:
@@ -277,7 +313,7 @@
         fix_inner(t0, put1)
 
         def own2(p, c):
-            for f, value in enumerate(lap(J1, p + 2, YO, 32)):
+            for f, value in enumerate(lap_z(J1, p + 2, Z[p])):
                 u = U[p, f]
                 a = S[p + XO, f, OWN, :] * u + D * value
                 J2[p + 2, f, OWN, :] = J1[p + 2, f, OWN, :] + H * a
@@ -286,7 +322,8 @@
                 U[p, f] = u + H * value
             return c
 
-        lax.fori_loop(0, 8, own2, 0)
+        faces_first(own2, J1)
+        inner(own2, J1)
 
         for copy in diag:
             copy.wait()
@@ -385,7 +422,7 @@
         raised = level == 1
 
         def own3(p, c):
-            for f, value in enumerate(lap(J2, p + 2, YO, 32)):
+            for f, value in enumerate(lap_z(J2, p + 2, Z[p])):
                 u, v8, v7 = U[p, f], J2[p + 2, f, OWN, :], J1[p + 2, f, OWN, :]
                 a8 = S[p + XO, f, OWN, :] * u + D * value
                 if last:
@@ -399,7 +436,8 @@
                     U[p, f] = u + H * value
             return c
 
-        lax.fori_loop(0, 8, own3, 0)
+        faces_first(own3, J2)
+        inner(own3, J2)
 
         for copy in diag1:
             copy.wait()
@@ -437,13 +475,12 @@
                 U[p, :, off(sl), :] = U[p, :, off(sl), :] + H * xv
 
         fix_faces(t2, put3)
-        if not last:
-            x0 = send_x(r + 1, 0, I0, 2, T0.at[r + 1])
         fix_inner(t2, put3)
         if not last:
             for i in range(4):
                 pack(i, False)
             diag = send_corners(r + 1, 3)
+            x0 = send_x(r + 1, 0, I0, 2, T0.at[r + 1])
             y0 = send_y(r + 1, 2, I0, 2, T0.at[r + 1])
 
 
@@ -453,7 +490,7 @@
     scratch = [vm(*alone)] * 6 + [vm(ROUNDS, *ext)] * 3 + [vm(*ext)] * 2 + [vm(*block)] * 3
     scratch += [vm(6, 2, 48, 128)] * 2 + [vm(12, 2, 24, 128)] * 2
     scratch += [vm(2, 2, 32, 128)] * 2 + [vm(8, 2, 8, 128)] * 2
-    scratch += [vm(4, 8, 8, 128), vm(ROUNDS, 4, 8, 8, 128), vm(2, 2, 8, 128), vm(2, 2, 8, 128)]
+    scratch += [vm(4, 8, 8, 128), vm(ROUNDS, 4, 8, 8, 128), vm(2, 2, 8, 128), vm(2, 2, 8, 128), vm(*block), pltpu.VMEM((256, 256), jnp.bfloat16)]
     scratch += [pltpu.SemaphoreType.DMA((6,)), pltpu.SemaphoreType.DMA((30,)), pltpu.SemaphoreType.DMA((50,))]
     out = jax.ShapeDtypeStruct((1, 8, 32, 256), F32)
     return pl.pallas_call(

time: 38.8 us -> 36.9 us (0.951)
  Pallas kernels: 36.7 us -> 34.8 us
    pallas_call x1, Pallas kernels: 36.7 us -> 34.8 us  [body(): pl.pallas_call(kernel, out_shape=(out, out), in_specs=[pl.BlockSpec(memor...]
where the time goes in v3:
time: 36.9 us; the launch traced here: 36.8 us
  Pallas kernels  34.8 us (94%)
  local copies, waits for them, and re-layouts  1.41 us (4%)
  between operations  0.64 us (2%)
    pallas_call x1, Pallas kernels, body(): pl.pallas_call(kernel, out_shape=(out, out), in_specs=[pl.BlockSpec(memor...  34.8 us
    unnamed x2, local copies, waits for them, and re-layouts  1.41 us

profile of v3, /device:TPU:1, one launch (start us, length us, event | category | flops | bytes accessed | tf_op | source)
XLA Modules:
  0.0 36.8 jit_solution(14598140372525598580)
XLA Ops:
  0.6 34.8 %shard_map.50 = (f32[1,8,32,256]{3,2,1,0:T(8,128)S(1)}, f32[1,8,32,256]{3,2,1,0:T(8,128)S(1)}) custom-call(f32[8,32,256]{2,1,0:T(8,128)} %u_hbm.1, f32[8,32,256]{2,1,0:T(8,128)} %v_hbm.1, f32[8,32,256]{2,1,0:T(8,128)} %s_hbm.1), custom_call_target="tpu_custom_call" | custom-call | tf_op jit(solution)/shard_map/pallas_call | solution.py:496
  35.4 0.7 %copy.7 = f32[1,8,32,256]{3,2,1,0:T(8,128)} copy(f32[1,8,32,256]{3,2,1,0:T(8,128)S(1)} %get-tuple-element.4) | data formatting | bytes 524288
  36.1 0.7 %copy.8 = f32[1,8,32,256]{3,2,1,0:T(8,128)} copy(f32[1,8,32,256]{3,2,1,0:T(8,128)S(1)} %get-tuple-element.5) | data formatting | bytes 524288

commit v4 on v3

--- a/solution.py
+++ b/solution.py
@@ -246,12 +246,15 @@
     def send_corners(r, n):
         return [send(r, 12 + i, cs.at[i, 0:n], cr.at[r, i, 0:n], *DIAG[i]) for i in range(4)]
 
+    def pack1(i):
+        near, _, sl = corner(*DIAG[i])
+        cs[i, 7] = pack2(halves(I1, near, 2, sl), DIAG[i][1])
+
     def send_corners1(r):
         copies = []
-        for i, (sx, sy) in enumerate(DIAG):
-            near, far, sl = corner(sx, sy)
-            cs[i, 7] = pack2(halves(I1, near, 2, sl), sy)
-            copies.append(send(r, 16 + i, cs.at[i, 7:8], cr.at[r, i, 7:8], sx, sy))
+        for i in range(4):
+            pack1(i)
+            copies.append(send(r, 16 + i, cs.at[i, 7:8], cr.at[r, i, 7:8], *DIAG[i]))
         return copies
 
     def unpack2(tile):
@@ -276,21 +279,27 @@
                     a, b, c, d = [S[q + XO, f, sl, :] for q in planes for sl in (slice(8, 16), slice(32, 40))]
                     i = rows(a.shape)
                     fs[k, f] = jnp.where(i < 2, a, jnp.where(i >= 6, b, jnp.where(i < 4, turn(c, 2), turn(d, 6))))
+            faces_first(start, IU)
+            inner(start, IU)
+            faces_first(alone1, I0)
             for i in range(4):
                 pack(i, True)
+                pack1(i)
+            inner(alone1, I0)
             pl.semaphore_wait(barrier, len(around))
             x0 = send_x(r, 0, I0, 2, t0)
             y0 = send_y(r, 2, I0, 2, t0)
             extra = send_x(r, 20, IU, 2, TU) + send_y(r, 22, IU, 2, TU)
-            diag = send_corners(r, 7)
+            diag = send_corners(r, 8)
             extra += send_x(r, 24, S, XO, S) + send_y(r, 26, S, XO, S)
             extra += [send(r, 28, fs.at[0], fr.at[0], 1, 0), send(r, 29, fs.at[1], fr.at[1], -1, 0)]
-            faces_first(start, IU)
-            inner(start, IU)
-        faces_first(alone1, I0)
-        diag1 = send_corners1(r)
-        x1 = send_x(r, 4, I1, 2, t1)
-        inner(alone1, I0)
+        if first:
+            x1, diag1 = send_x(r, 4, I1, 2, t1), []
+        else:
+            faces_first(alone1, I0)
+            diag1 = send_corners1(r)
+            x1 = send_x(r, 4, I1, 2, t1)
+            inner(alone1, I0)
         y1 = send_y(r, 6, I1, 2, t1)
         faces_first(alone2, I1)
         x2 = send_x(r, 8, I2, 2, t2)

time: 36.9 us -> 36.8 us (level)
  no operation moved by 1% of the time
where the time goes in v4:
time: 36.8 us; the launch traced here: 36.7 us
  Pallas kernels  34.7 us (94%)
  local copies, waits for them, and re-layouts  1.41 us (4%)
  between operations  0.64 us (2%)
    pallas_call x1, Pallas kernels, body(): pl.pallas_call(kernel, out_shape=(out, out), in_specs=[pl.BlockSpec(memor...  34.7 us
    unnamed x2, local copies, waits for them, and re-layouts  1.41 us

profile of v4, /device:TPU:1, one launch (start us, length us, event | category | flops | bytes accessed | tf_op | source)
XLA Modules:
  0.0 36.7 jit_solution(132468759001706695)
XLA Ops:
  0.6 34.7 %shard_map.50 = (f32[1,8,32,256]{3,2,1,0:T(8,128)S(1)}, f32[1,8,32,256]{3,2,1,0:T(8,128)S(1)}) custom-call(f32[8,32,256]{2,1,0:T(8,128)} %u_hbm.1, f32[8,32,256]{2,1,0:T(8,128)} %v_hbm.1, f32[8,32,256]{2,1,0:T(8,128)} %s_hbm.1), custom_call_target="tpu_custom_call" | custom-call | tf_op jit(solution)/shard_map/pallas_call | solution.py:505
  35.3 0.7 %copy.7 = f32[1,8,32,256]{3,2,1,0:T(8,128)} copy(f32[1,8,32,256]{3,2,1,0:T(8,128)S(1)} %get-tuple-element.4) | data formatting | bytes 524288
  36.0 0.7 %copy.8 = f32[1,8,32,256]{3,2,1,0:T(8,128)} copy(f32[1,8,32,256]{3,2,1,0:T(8,128)S(1)} %get-tuple-element.5) | data formatting | bytes 524288
